TPU v7x, 512 devices: a whole 4x8x8 slice. The times are simulated.
512 devices in a mesh: section: 4 (over y_lo), row: 16 (over z, core), col: 8 (over y_hi, x).
Axes of the slice: x: 4, y: 8 (y_hi: 2, y_lo: 4; y = y_hi * 4 + y_lo), z: 8, core: 2. Of those that a mesh axis runs over, the one named last changes fastest.
Arguments:
- section_input: bfloat16 [4, 2, 128, 128, 128], P('section', None, 'row', 'col'), may hold values from -6 to 6
- first_pre: bfloat16 [4, 2, 128, 128, 128], P('section', None, 'row', 'col'), may hold values from -6 to 6
- second_pre: bfloat16 [4, 2, 128, 128, 128], P('section', None, 'row', 'col'), may hold values from -6 to 6
- out_grad: bfloat16 [2, 128, 128, 128], P(None, 'row', 'col'), may hold values from -6 to 6
- kernels: bfloat16 [4, 2, 3, 3, 128, 128], P('section'), may hold values from -0.1875 to 0.1875
- bn_scale: float32 [4, 2, 128], P('section'), may hold values from 0.5 to 2
- bn_shift: float32 [4, 2, 128], P('section'), may hold values from -3 to 3
Outputs:
- input_grad: bfloat16 [4, 2, 128, 128, 128], P('section', None, 'row', 'col')
- filter_grad: float32 [4, 2, 3, 3, 128, 128], P('section')
All inputs are finite; a program needn't handle non-finite values.
Results may differ from a plain program's by a relative error of at most 0.013.
Values may be sent and summed in bfloat16 or wider, within the bound.
No kernel may reach another device: no remote copies, remote signals or barrier semaphores. Data moves between devices by JAX's collectives and lax.ppermute only.
A program may use at most 64 MiB of HBM per device.

v0:
```python
import jax
import jax.numpy as jnp
from jax import lax
from jax.sharding import Mesh
from jax.sharding import PartitionSpec as P

ROW = ("row_0", "row_1")
COL = ("col_0", "col_1")
NEAR = ("row_1", "col_1")
FAR = ("row_0", "col_0")


def with_halo(cells, axis, dim, width):
    count = lax.axis_size(axis)
    size = cells.shape[dim]
    head = lax.slice_in_dim(cells, 0, width, axis=dim)
    tail = lax.slice_in_dim(cells, size - width, size, axis=dim)
    before = lax.ppermute(tail, axis, [(i, i + 1) for i in range(count - 1)])
    after = lax.ppermute(head, axis, [(i + 1, i) for i in range(count - 1)])
    return jnp.concatenate([before, cells, after], axis=dim)


def crop(field, cut):
    if cut == 0:
        return field
    return field[:, cut:-cut, cut:-cut]


def correlate(padded, kernel):
    return lax.conv_general_dilated(
        padded,
        kernel,
        (1, 1),
        "VALID",
        dimension_numbers=("NHWC", "HWIO", "NHWC"),
        preferred_element_type=jnp.float32,
    )


def flip_kernel(kernel):
    return jnp.transpose(jnp.flip(kernel, (0, 1)), (0, 1, 3, 2))


def kernel_grad(cells, padded):
    rows_here, cols_here = (cells.shape[1], cells.shape[2])
    windows = jnp.stack(
        [
            padded[:, 2 - i : 2 - i + rows_here, 2 - j : 2 - j + cols_here]
            for i in range(3)
            for j in range(3)
        ]
    )
    return jnp.einsum("mhwc,kmhwd->kcd", cells, windows, preferred_element_type=jnp.float32)


def sum_of_blocks(blocks, axes):
    parts = lax.all_to_all(blocks, axes, 0, 0, tiled=True)
    return jnp.sum(parts.astype(jnp.float32), axis=0)


def copies(block, axes):
    count = lax.axis_size(axes)
    return lax.all_to_all(
        jnp.broadcast_to(block[None], (count, *block.shape)), axes, 0, 0, tiled=True
    )


def total_of(x, factor):
    near, stack = (lax.axis_size(NEAR), lax.axis_size("row_0"))
    width = x.shape[-1]
    lines = x.astype(jnp.bfloat16).reshape(near, -1, width)
    part = sum_of_blocks(lines, NEAR).astype(jnp.bfloat16).reshape(stack, 1, -1, width)
    twice = jnp.broadcast_to(part, (stack, lax.axis_size("col_0"), *part.shape[2:]))
    own = sum_of_blocks(twice.reshape(-1, *part.shape[2:]), FAR)
    own = (own * factor).astype(jnp.bfloat16)
    part = lax.all_gather(own, "row_0", axis=0, tiled=True)
    return copies(part, NEAR).reshape(x.shape).astype(jnp.float32)


def on_device(section_input, first_pre, second_pre, out_grad, kernels, bn_scale, bn_shift):
    section_index = lax.axis_index("section")
    sections = lax.axis_size("section")
    last = section_index == sections - 1
    micros, rows_here, cols_here, width = out_grad.shape
    inputs = section_input[0]
    kernel = kernels[0]
    scales = bn_scale[0]
    shifts = bn_shift[0]
    first_norm = scales[0] * first_pre[0].astype(jnp.float32) + shifts[0]
    first_act = jnp.maximum(first_norm, 0.0).astype(jnp.bfloat16)
    second_norm = scales[1] * second_pre[0].astype(jnp.float32) + shifts[1]
    alive = second_norm + inputs.astype(jnp.float32) > 0
    one = jnp.ones((), jnp.bfloat16)
    zero = jnp.zeros((), jnp.bfloat16)
    passed = jnp.where(alive, jnp.where(last, out_grad, one), zero)
    first_on = jnp.where(first_norm > 0, one, zero)
    depth = 2 * sections
    masks = jnp.stack([passed, first_on])
    masks = with_halo(masks, COL, 3, depth)
    masks = with_halo(masks, ROW, 2, depth)
    passed, first_on = (masks[0], masks[1])
    flip_first = flip_kernel(kernel[0])
    flip_second = flip_kernel(kernel[1])

    def unit(incoming, reach):
        masked = crop(passed, depth - reach - 2)
        if incoming is not None:
            masked = masked * incoming
        masked = masked.astype(jnp.float32)
        second_grad = (scales[1] * masked).astype(jnp.bfloat16)
        act_grad = correlate(second_grad, flip_second)
        on = crop(first_on, depth - reach - 1).astype(jnp.float32)
        first_grad = (scales[0] * (act_grad * on)).astype(jnp.bfloat16)
        result = crop(masked, 2) + correlate(first_grad, flip_first)
        return (result.astype(jnp.bfloat16), first_grad, second_grad)

    received = None
    own_incoming = jnp.where(last, one, zero)
    for step in range(sections - 1):
        reach = 2 * (sections - 1 - step)
        result, _, _ = unit(received, reach)
        received = lax.ppermute(result, "section", [(sections - 1 - step, sections - 2 - step)])
        own_incoming = own_incoming + crop(received, reach - 2)
    input_grad, first_grad, second_grad = unit(own_incoming, 0)
    partial = jnp.stack(
        [kernel_grad(inputs, first_grad), kernel_grad(first_act, crop(second_grad, 1))]
    )
    pixels = micros * rows_here * lax.axis_size(ROW) * cols_here * lax.axis_size(COL)
    factor = 1.0 / jnp.sqrt(jnp.float32(pixels))
    total = total_of(partial, factor).reshape(2, 3, 3, width, width)
    return (input_grad[None], total[None])


def solution(mesh):
    split = Mesh(
        mesh.devices.reshape(mesh.shape["section"], 8, 2, 2, 4),
        ("section", "row_0", "row_1", "col_0", "col_1"),
    )
    in_specs = (
        P("section", None, ROW, COL, None),
        P("section", None, ROW, COL, None),
        P("section", None, ROW, COL, None),
        P(None, ROW, COL, None),
        P("section", None, None, None, None, None),
        P("section", None, None),
        P("section", None, None),
    )
    out_specs = (P("section", None, ROW, COL, None), P("section", None, None, None, None, None))
    return jax.shard_map(
        on_device, mesh=split, in_specs=in_specs, out_specs=out_specs, check_vma=False
    )
```

profile of v0, /device:TPU:1, one launch (start us, length us, event | category | flops | bytes accessed | tf_op | source)
XLA Modules:
  0.0 150.6 jit_solution(10677023709551831681)
XLA Ops:
  1.4 0.9 fusion.103
  2.3 1.0 fusion.104
  3.3 3.9 %collective-permute-start = (bf16[2,2,8,8,128]{4,3,1,2,0:T(8,128)(2,1)S(1)}, bf16[2,2,8,8,128]{4,3,1,2,0:T(8,128)(2,1)S(1)}, u32[]{:S(2)}, u32[]{:S(2)}) collective-permute-start(bf16[2,2,8,8,128]{4,3,1,2,0:T(8,128)(2,1)S(1)} %get-tuple-element.19), channel_id=1, source_target_pairs={{0,1},{1,2},{2,3},{3,4},{4,5},{5,6},{6,7},{8,9},{9,10},{10,11},{11... | collective-permute-start | bytes 196616 | tf_op jit(solution)/shard_map/ppermute | solution.py:18
  7.2 1.3 collective-permute-start.1
  8.5 3.7 %collective-permute-done.1 = bf16[2,2,8,8,128]{4,3,1,2,0:T(8,128)(2,1)S(1)} collective-permute-done((bf16[2,2,8,8,128]{4,3,1,2,0:T(8,128)(2,1)S(1)}, bf16[2,2,8,8,128]{4,3,1,2,0:T(8,128)(2,1)S(1)}, u32[]{:S(2)}, u32[]{:S(2)}) %collective-permute-start.1) | collective-permute-done | bytes 65568 | tf_op jit(solution)/shard_map/ppermute | solution.py:19
  12.3 7.3 %collective-permute-start.3 = (bf16[2,2,8,32,128]{4,3,1,2,0:T(8,128)(2,1)S(1)}, bf16[2,2,8,32,128]{4,3,1,2,0:T(8,128)(2,1)S(1)}, u32[]{:S(2)}, u32[]{:S(2)}) collective-permute-start(bf16[2,2,8,32,128]{4,3,1,2,0:T(8,128)(2,1)S(1)} %pad_maximum_fusion.2), channel_id=1, source_target_pairs={{8,0},{16,8},{24,16},{32,24},{40,32},{48,40},{56,48},{64,56},{72,6... | collective-permute-start | bytes 786440 | tf_op jit(solution)/shard_map/ppermute | solution.py:19
  19.5 1.9 %collective-permute-start.2 = (bf16[2,2,8,32,128]{4,3,1,2,0:T(8,128)(2,1)S(1)}, bf16[2,2,8,32,128]{4,3,1,2,0:T(8,128)(2,1)S(1)}, u32[]{:S(2)}, u32[]{:S(2)}) collective-permute-start(bf16[2,2,8,32,128]{4,3,1,2,0:T(8,128)(2,1)S(1)} %pad_maximum_fusion.2), channel_id=1, source_target_pairs={{0,8},{8,16},{16,24},{24,32},{32,40},{40,48},{48,56},{56,64},{64,7... | collective-permute-start | bytes 786440 | tf_op jit(solution)/shard_map/ppermute | solution.py:18
  21.4 0.8 collective-permute-done.3
  22.3 2.4 %collective-permute-done.2 = bf16[2,2,8,32,128]{4,3,1,2,0:T(8,128)(2,1)S(1)} collective-permute-done((bf16[2,2,8,32,128]{4,3,1,2,0:T(8,128)(2,1)S(1)}, bf16[2,2,8,32,128]{4,3,1,2,0:T(8,128)(2,1)S(1)}, u32[]{:S(2)}, u32[]{:S(2)}) %collective-permute-start.2) | collective-permute-done | bytes 262176 | tf_op jit(solution)/shard_map/ppermute | solution.py:18
  25.3 0.9 copy-done.2
  26.2 1.0 convolution_select_fusion
  28.4 0.9 convolution_select_fusion.1
  31.0 0.9 convolution_select_fusion.2
  32.8 0.8 convolution_select_fusion.3
  37.6 1.3 collective-permute-start.6
  38.9 15.0 %collective-permute-done.6 = bf16[2,12,20,128]{3,2,0,1:T(8,128)(2,1)S(1)} collective-permute-done((bf16[2,12,20,128]{3,2,0,1:T(8,128)(2,1)S(1)}, bf16[2,12,20,128]{3,2,0,1:T(8,128)(2,1)S(1)}, u32[]{:S(2)}, u32[]{:S(2)}) %collective-permute-start.6) | collective-permute-done | bytes 122912 | tf_op jit(solution)/shard_map/ppermute | solution.py:122
  57.1 23.5 %all_to_all.15 = bf16[8,288,128]{2,1,0:T(8,128)(2,1)S(1)} all-to-all(bf16[8,288,128]{2,1,0:T(8,128)(2,1)S(1)} %bitcast.307), channel_id=1, replica_groups=mesh['section'=4,'row_0'=8,'row_1'=2,'col_0'=2,'col_1'=4] {'row_1','col_1'}, dimensions={0} | all-to-all | bytes 1179648 | tf_op jit(solution)/shard_map/all_to_all | solution.py:57
  81.4 15.1 %all-to-all-start.1 = ((bf16[16,36,128]{2,1,0:T(8,128)(2,1)}), bf16[16,36,128]{2,1,0:T(8,128)(2,1)S(1)}, u32[]{:S(2)}, u32[]{:S(2)}) async-start(bf16[16,36,128]{2,1,0:T(8,128)(2,1)} %bitcast.91), calls=%async_computation.1 | async-start | bytes 327680 | tf_op jit(solution)/shard_map/all_to_all | solution.py:57
  96.7 12.0 %all-to-all-done.1 = bf16[16,36,128]{2,1,0:T(8,128)(2,1)S(1)} async-done(((bf16[16,36,128]{2,1,0:T(8,128)(2,1)}), bf16[16,36,128]{2,1,0:T(8,128)(2,1)S(1)}, u32[]{:S(2)}, u32[]{:S(2)}) %all-to-all-start.1) | async-done | bytes 147488 | tf_op jit(solution)/shard_map/all_to_all | solution.py:57
  108.8 18.5 %all-gather = bf16[8,36,128]{2,1,0:T(8,128)(2,1)S(1)} all-gather(bf16[1,36,128]{2,1,0:T(8,128)(2,1)S(1)} %fusion.133), channel_id=1, replica_groups=mesh['section'=4,'row_0'=8,'row_1'=2,'col_0'=2,'col_1'=4] {'row_0'}, dimensions={0}, use_global_device_ids=true | all-gather | bytes 82944 | tf_op jit(solution)/shard_map/all_gather | solution.py:76
  127.3 0.9 broadcast_in_dim.39
  128.2 11.2 %all-to-all-start.2 = ((bf16[8,288,128]{2,1,0:T(8,128)(2,1)}), bf16[8,288,128]{2,1,0:T(8,128)(2,1)S(1)}, u32[]{:S(2)}, u32[]{:S(2)}) async-start(bf16[8,288,128]{2,1,0:T(8,128)(2,1)} %broadcast_in_dim.39), calls=%async_computation.2 | async-start | bytes 1179648 | tf_op jit(solution)/shard_map/all_to_all | solution.py:63
  140.7 8.7 %all-to-all-done.2 = bf16[8,288,128]{2,1,0:T(8,128)(2,1)S(1)} async-done(((bf16[8,288,128]{2,1,0:T(8,128)(2,1)}), bf16[8,288,128]{2,1,0:T(8,128)(2,1)S(1)}, u32[]{:S(2)}, u32[]{:S(2)}) %all-to-all-start.2) | async-done | bytes 589856 | tf_op jit(solution)/shard_map/all_to_all | solution.py:63
  149.4 1.1 convert.17
  (116 shorter events, 14.1 us)
Async XLA Ops:
  3.3 5.3 %collective-permute-start = (bf16[2,2,8,8,128]{4,3,1,2,0:T(8,128)(2,1)S(1)}, bf16[2,2,8,8,128]{4,3,1,2,0:T(8,128)(2,1)S(1)}, u32[]{:S(2)}, u32[]{:S(2)}) collective-permute-start(bf16[2,2,8,8,128]{4,3,1,2,0:T(8,128)(2,1)S(1)} %get-tuple-element.19), channel_id=1, source_target_pairs={{0,1},{1,2},{2,3},{3,4},{4,5},{5,6},{6,7},{8,9},{9,10},{10,11},{11... | collective-permute-start | bytes 196616 | tf_op jit(solution)/shard_map/ppermute | solution.py:18
  7.2 5.0 %collective-permute-start.1 = (bf16[2,2,8,8,128]{4,3,1,2,0:T(8,128)(2,1)S(1)}, bf16[2,2,8,8,128]{4,3,1,2,0:T(8,128)(2,1)S(1)}, u32[]{:S(2)}, u32[]{:S(2)}) collective-permute-start(bf16[2,2,8,8,128]{4,3,1,2,0:T(8,128)(2,1)S(1)} %get-tuple-element.20), channel_id=1, source_target_pairs={{1,0},{2,1},{3,2},{4,3},{5,4},{6,5},{7,6},{9,8},{10,9},{11,10},{12... | collective-permute-start | bytes 196616 | tf_op jit(solution)/shard_map/ppermute | solution.py:19
  12.3 10.0 %collective-permute-start.3 = (bf16[2,2,8,32,128]{4,3,1,2,0:T(8,128)(2,1)S(1)}, bf16[2,2,8,32,128]{4,3,1,2,0:T(8,128)(2,1)S(1)}, u32[]{:S(2)}, u32[]{:S(2)}) collective-permute-start(bf16[2,2,8,32,128]{4,3,1,2,0:T(8,128)(2,1)S(1)} %pad_maximum_fusion.2), channel_id=1, source_target_pairs={{8,0},{16,8},{24,16},{32,24},{40,32},{48,40},{56,48},{64,56},{72,6... | collective-permute-start | bytes 786440 | tf_op jit(solution)/shard_map/ppermute | solution.py:19
  19.5 5.2 %collective-permute-start.2 = (bf16[2,2,8,32,128]{4,3,1,2,0:T(8,128)(2,1)S(1)}, bf16[2,2,8,32,128]{4,3,1,2,0:T(8,128)(2,1)S(1)}, u32[]{:S(2)}, u32[]{:S(2)}) collective-permute-start(bf16[2,2,8,32,128]{4,3,1,2,0:T(8,128)(2,1)S(1)} %pad_maximum_fusion.2), channel_id=1, source_target_pairs={{0,8},{8,16},{16,24},{24,32},{32,40},{40,48},{48,56},{56,64},{64,7... | collective-permute-start | bytes 786440 | tf_op jit(solution)/shard_map/ppermute | solution.py:18
  25.1 1.1 copy-start.2
  25.2 1.1 copy-start.10
  27.7 0.7 copy-start.9
  29.7 0.7 collective-permute-start.4
  30.4 0.7 copy-start.8
  32.2 0.7 copy-start.7
  34.1 1.1 copy-start.6
  34.2 0.7 collective-permute-start.5
  35.9 0.8 copy-start.5
  37.6 16.4 %collective-permute-start.6 = (bf16[2,12,20,128]{3,2,0,1:T(8,128)(2,1)S(1)}, bf16[2,12,20,128]{3,2,0,1:T(8,128)(2,1)S(1)}, u32[]{:S(2)}, u32[]{:S(2)}) collective-permute-start(bf16[2,12,20,128]{3,2,0,1:T(8,128)(2,1)S(1)} %fusion.53), channel_id=1, source_target_pairs={{128,0},{129,1},{130,2},{131,3},{132,4},{133,5},{134,6},{135,7},{1... | collective-permute-start | bytes 368648 | tf_op jit(solution)/shard_map/ppermute | solution.py:122
  38.9 15.7 %copy-start.4 = (pred[16,3]{0,1:T(4,128)(4,1)S(1)}, pred[16,3]{0,1:T(4,128)(4,1)}, u32[]{:S(2)}) copy-start(pred[16,3]{0,1:T(4,128)(4,1)} %constant.62) | copy-start | bytes 148
  55.3 0.8 copy-start.1
  55.7 1.1 copy-start
  81.4 27.3 %all-to-all-start.1 = ((bf16[16,36,128]{2,1,0:T(8,128)(2,1)}), bf16[16,36,128]{2,1,0:T(8,128)(2,1)S(1)}, u32[]{:S(2)}, u32[]{:S(2)}) async-start(bf16[16,36,128]{2,1,0:T(8,128)(2,1)} %bitcast.91), calls=%async_computation.1 | async-start | bytes 327680 | tf_op jit(solution)/shard_map/all_to_all | solution.py:57
  127.3 12.3 %copy-start.3 = (pred[16,3]{0,1:T(4,128)(4,1)S(1)}, pred[16,3]{0,1:T(4,128)(4,1)}, u32[]{:S(2)}) copy-start(pred[16,3]{0,1:T(4,128)(4,1)} %constant.61) | copy-start | bytes 148
  128.2 21.2 %all-to-all-start.2 = ((bf16[8,288,128]{2,1,0:T(8,128)(2,1)}), bf16[8,288,128]{2,1,0:T(8,128)(2,1)S(1)}, u32[]{:S(2)}, u32[]{:S(2)}) async-start(bf16[8,288,128]{2,1,0:T(8,128)(2,1)} %broadcast_in_dim.39), calls=%async_computation.2 | async-start | bytes 1179648 | tf_op jit(solution)/shard_map/all_to_all | solution.py:63
where the time goes:
time: 151 us
  starting transfers between devices  43.3 us (29%)
  waiting for transfers between devices  42.7 us (28%)
  blocking collectives  42 us (28%)
  local copies, waits for them, and re-layouts  9.26 us (6%)
  matrix products  6.13 us (4%)
  other arithmetic  5.69 us (4%)
    all_to_all x1, blocking collectives, sum_of_blocks(): parts = lax.all_to_all(blocks, axes, 0, 0, tiled=True)  23.5 us
    all_gather x1, blocking collectives, total_of(): part = lax.all_gather(own, 'row_0', axis=0, tiled=True)  18.5 us
    all_to_all x1, starting transfers between devices, sum_of_blocks(): parts = lax.all_to_all(blocks, axes, 0, 0, tiled=True)  15.1 us
    ppermute x3, waiting for transfers between devices, on_device(): lax.ppermute(result, 'section', [(sections - 1 - step, sections - 2 - ste...  15 us
    all_to_all x1, waiting for transfers between devices, sum_of_blocks(): parts = lax.all_to_all(blocks, axes, 0, 0, tiled=True)  12 us
    all_to_all x1, starting transfers between devices, copies(): lax.all_to_all(jnp.broadcast_to(block[None], (count, *block.shape)), axes...  11.2 us
    all_to_all x1, waiting for transfers between devices, copies(): lax.all_to_all(jnp.broadcast_to(block[None], (count, *block.shape)), axes...  8.7 us
    ppermute x2, starting transfers between devices, with_halo(): after = lax.ppermute(head, axis, [(i + 1, i) for i in range(count - 1)])  8.55 us
  transfers between devices with their start and end apart: 9, of which 6 were waited for; matrix products, arithmetic and copies ran while one was open for 1% of the time, Pallas kernels for 0%

commit v1 on v0

--- a/solution.py
+++ b/solution.py
@@ -73,7 +73,9 @@
     twice = jnp.broadcast_to(part, (stack, lax.axis_size("col_0"), *part.shape[2:]))
     own = sum_of_blocks(twice.reshape(-1, *part.shape[2:]), FAR)
     own = (own * factor).astype(jnp.bfloat16)
-    part = lax.all_gather(own, "row_0", axis=0, tiled=True)
+    part = jnp.concatenate(
+        lax.all_to_all(jnp.stack([own] * lax.axis_size("row_0")), "row_0", 0, 0), axis=0
+    )
     return copies(part, NEAR).reshape(x.shape).astype(jnp.float32)
 
 

time: 151 us -> 138 us (0.914)
  starting transfers between devices: 43.3 us -> 26.6 us
  blocking collectives: 42 us -> 50.6 us
  waiting for transfers between devices: 42.7 us -> 37.8 us
    all_to_all x1 -> x2, blocking collectives: 23.5 us -> 50.6 us  [sum_of_blocks(): parts = lax.all_to_all(blocks, axes, 0, 0, tiled=True)]
    all_gather x1 -> x0, blocking collectives: 18.5 us -> none  [total_of(): part = lax.all_gather(own, 'row_0', axis=0, tiled=True)]
    all_to_all x1, starting transfers between devices: 15.1 us -> 3.36 us  [total_of(): lax.all_to_all(jnp.stack([own] * lax.axis_size('row_0')), 'row_0', 0, 0)]
    all_to_all x1, starting transfers between devices: 11.2 us -> 6.21 us  [copies(): lax.all_to_all(jnp.broadcast_to(block[None], (count, *block.shape)), axes...]
    all_to_all x1, waiting for transfers between devices: 12 us -> 7.07 us  [total_of(): lax.all_to_all(jnp.stack([own] * lax.axis_size('row_0')), 'row_0', 0, 0)]
    unnamed x43 -> x42, local copies, waits for them, and re-layouts: 3.88 us -> 3.86 us
where the time goes in v1:
time: 138 us
  blocking collectives  50.6 us (37%)
  waiting for transfers between devices  37.8 us (27%)
  starting transfers between devices  26.6 us (19%)
  local copies, waits for them, and re-layouts  9.25 us (7%)
  matrix products  6.12 us (4%)
  other arithmetic  5.69 us (4%)
  between operations  1.46 us (1%)
    all_to_all x2, blocking collectives, sum_of_blocks(): parts = lax.all_to_all(blocks, axes, 0, 0, tiled=True)  50.6 us
    ppermute x3, waiting for transfers between devices, on_device(): lax.ppermute(result, 'section', [(sections - 1 - step, sections - 2 - ste...  15 us
    all_to_all x1, waiting for transfers between devices, copies(): lax.all_to_all(jnp.broadcast_to(block[None], (count, *block.shape)), axes...  8.7 us
    ppermute x2, starting transfers between devices, with_halo(): after = lax.ppermute(head, axis, [(i + 1, i) for i in range(count - 1)])  8.55 us
    all_to_all x1, waiting for transfers between devices, total_of(): lax.all_to_all(jnp.stack([own] * lax.axis_size('row_0')), 'row_0', 0, 0)  7.07 us
    all_to_all x1, starting transfers between devices, copies(): lax.all_to_all(jnp.broadcast_to(block[None], (count, *block.shape)), axes...  6.21 us
    ppermute x2, starting transfers between devices, with_halo(): before = lax.ppermute(tail, axis, [(i, i + 1) for i in range(count - 1)])  5.86 us
    conv_general_dilated x8, matrix products, correlate(): lax.conv_general_dilated(padded, kernel, (1, 1), 'VALID', dimension_numbe...  5.53 us
  transfers between devices with their start and end apart: 9, of which 6 were waited for; matrix products, arithmetic and copies ran while one was open for 1% of the time, Pallas kernels for 0%

profile of v1, /device:TPU:1, one launch (start us, length us, event | category | flops | bytes accessed | tf_op | source)
XLA Modules:
  0.0 137.6 jit_solution(5787637013592487347)
XLA Ops:
  1.4 0.9 fusion.103
  2.3 1.0 fusion.104
  3.3 3.9 %collective-permute-start = (bf16[2,2,8,8,128]{4,3,1,2,0:T(8,128)(2,1)S(1)}, bf16[2,2,8,8,128]{4,3,1,2,0:T(8,128)(2,1)S(1)}, u32[]{:S(2)}, u32[]{:S(2)}) collective-permute-start(bf16[2,2,8,8,128]{4,3,1,2,0:T(8,128)(2,1)S(1)} %get-tuple-element.17), channel_id=1, source_target_pairs={{0,1},{1,2},{2,3},{3,4},{4,5},{5,6},{6,7},{8,9},{9,10},{10,11},{11... | collective-permute-start | bytes 196616 | tf_op jit(solution)/shard_map/ppermute | solution.py:18
  7.2 1.3 collective-permute-start.1
  8.5 3.7 %collective-permute-done.1 = bf16[2,2,8,8,128]{4,3,1,2,0:T(8,128)(2,1)S(1)} collective-permute-done((bf16[2,2,8,8,128]{4,3,1,2,0:T(8,128)(2,1)S(1)}, bf16[2,2,8,8,128]{4,3,1,2,0:T(8,128)(2,1)S(1)}, u32[]{:S(2)}, u32[]{:S(2)}) %collective-permute-start.1) | collective-permute-done | bytes 65568 | tf_op jit(solution)/shard_map/ppermute | solution.py:19
  12.3 7.3 %collective-permute-start.3 = (bf16[2,2,8,32,128]{4,3,1,2,0:T(8,128)(2,1)S(1)}, bf16[2,2,8,32,128]{4,3,1,2,0:T(8,128)(2,1)S(1)}, u32[]{:S(2)}, u32[]{:S(2)}) collective-permute-start(bf16[2,2,8,32,128]{4,3,1,2,0:T(8,128)(2,1)S(1)} %pad_maximum_fusion.2), channel_id=1, source_target_pairs={{8,0},{16,8},{24,16},{32,24},{40,32},{48,40},{56,48},{64,56},{72,6... | collective-permute-start | bytes 786440 | tf_op jit(solution)/shard_map/ppermute | solution.py:19
  19.5 1.9 %collective-permute-start.2 = (bf16[2,2,8,32,128]{4,3,1,2,0:T(8,128)(2,1)S(1)}, bf16[2,2,8,32,128]{4,3,1,2,0:T(8,128)(2,1)S(1)}, u32[]{:S(2)}, u32[]{:S(2)}) collective-permute-start(bf16[2,2,8,32,128]{4,3,1,2,0:T(8,128)(2,1)S(1)} %pad_maximum_fusion.2), channel_id=1, source_target_pairs={{0,8},{8,16},{16,24},{24,32},{32,40},{40,48},{48,56},{56,64},{64,7... | collective-permute-start | bytes 786440 | tf_op jit(solution)/shard_map/ppermute | solution.py:18
  21.4 0.8 collective-permute-done.3
  22.3 2.4 %collective-permute-done.2 = bf16[2,2,8,32,128]{4,3,1,2,0:T(8,128)(2,1)S(1)} collective-permute-done((bf16[2,2,8,32,128]{4,3,1,2,0:T(8,128)(2,1)S(1)}, bf16[2,2,8,32,128]{4,3,1,2,0:T(8,128)(2,1)S(1)}, u32[]{:S(2)}, u32[]{:S(2)}) %collective-permute-start.2) | collective-permute-done | bytes 262176 | tf_op jit(solution)/shard_map/ppermute | solution.py:18
  25.3 0.9 copy-done.2
  26.2 1.0 convolution_select_fusion
  28.4 0.9 convolution_select_fusion.1
  31.0 0.9 convolution_select_fusion.2
  32.8 0.8 convolution_select_fusion.3
  37.6 1.3 collective-permute-start.6
  38.9 15.0 %collective-permute-done.6 = bf16[2,12,20,128]{3,2,0,1:T(8,128)(2,1)S(1)} collective-permute-done((bf16[2,12,20,128]{3,2,0,1:T(8,128)(2,1)S(1)}, bf16[2,12,20,128]{3,2,0,1:T(8,128)(2,1)S(1)}, u32[]{:S(2)}, u32[]{:S(2)}) %collective-permute-start.6) | collective-permute-done | bytes 122912 | tf_op jit(solution)/shard_map/ppermute | solution.py:124
  57.1 23.5 %all_to_all.20 = bf16[8,288,128]{2,1,0:T(8,128)(2,1)S(1)} all-to-all(bf16[8,288,128]{2,1,0:T(8,128)(2,1)S(1)} %bitcast.305), channel_id=1, replica_groups=mesh['section'=4,'row_0'=8,'row_1'=2,'col_0'=2,'col_1'=4] {'row_1','col_1'}, dimensions={0} | all-to-all | bytes 1179648 | tf_op jit(solution)/shard_map/all_to_all | solution.py:57
  80.7 27.1 %all_to_all.21 = bf16[16,36,128]{2,1,0:T(8,128)(2,1)S(1)} all-to-all(bf16[16,36,128]{2,1,0:T(8,128)(2,1)S(1)} %bitcast.321), channel_id=1, replica_groups=mesh['section'=4,'row_0'=8,'row_1'=2,'col_0'=2,'col_1'=4] {'row_0','col_0'}, dimensions={0} | all-to-all | bytes 294912 | tf_op jit(solution)/shard_map/all_to_all | solution.py:57
  108.6 3.4 %all-to-all-start.2 = ((bf16[8,36,128]{2,1,0:T(8,128)(2,1)}), bf16[8,36,128]{2,1,0:T(8,128)(2,1)S(1)}, u32[]{:S(2)}, u32[]{:S(2)}) async-start(bf16[8,36,128]{2,1,0:T(8,128)(2,1)} %stack.115), calls=%async_computation.2 | async-start | bytes 163840 | tf_op jit(solution)/shard_map/all_to_all | solution.py:77
  112.2 7.1 %all-to-all-done.2 = bf16[8,36,128]{2,1,0:T(8,128)(2,1)S(1)} async-done(((bf16[8,36,128]{2,1,0:T(8,128)(2,1)}), bf16[8,36,128]{2,1,0:T(8,128)(2,1)S(1)}, u32[]{:S(2)}, u32[]{:S(2)}) %all-to-all-start.2) | async-done | bytes 73760 | tf_op jit(solution)/shard_map/all_to_all | solution.py:77
  119.3 0.9 broadcast_in_dim.41
  120.2 6.2 %all-to-all-start.3 = ((bf16[8,288,128]{2,1,0:T(8,128)(2,1)}), bf16[8,288,128]{2,1,0:T(8,128)(2,1)S(1)}, u32[]{:S(2)}, u32[]{:S(2)}) async-start(bf16[8,288,128]{2,1,0:T(8,128)(2,1)} %broadcast_in_dim.41), calls=%async_computation.3 | async-start | bytes 1179648 | tf_op jit(solution)/shard_map/all_to_all | solution.py:63
  127.7 8.7 %all-to-all-done.3 = bf16[8,288,128]{2,1,0:T(8,128)(2,1)S(1)} async-done(((bf16[8,288,128]{2,1,0:T(8,128)(2,1)}), bf16[8,288,128]{2,1,0:T(8,128)(2,1)S(1)}, u32[]{:S(2)}, u32[]{:S(2)}) %all-to-all-start.3) | async-done | bytes 589856 | tf_op jit(solution)/shard_map/all_to_all | solution.py:63
  136.4 1.1 convert.17
  (117 shorter events, 14.1 us)
Async XLA Ops:
  3.3 5.3 %collective-permute-start = (bf16[2,2,8,8,128]{4,3,1,2,0:T(8,128)(2,1)S(1)}, bf16[2,2,8,8,128]{4,3,1,2,0:T(8,128)(2,1)S(1)}, u32[]{:S(2)}, u32[]{:S(2)}) collective-permute-start(bf16[2,2,8,8,128]{4,3,1,2,0:T(8,128)(2,1)S(1)} %get-tuple-element.17), channel_id=1, source_target_pairs={{0,1},{1,2},{2,3},{3,4},{4,5},{5,6},{6,7},{8,9},{9,10},{10,11},{11... | collective-permute-start | bytes 196616 | tf_op jit(solution)/shard_map/ppermute | solution.py:18
  7.2 5.0 %collective-permute-start.1 = (bf16[2,2,8,8,128]{4,3,1,2,0:T(8,128)(2,1)S(1)}, bf16[2,2,8,8,128]{4,3,1,2,0:T(8,128)(2,1)S(1)}, u32[]{:S(2)}, u32[]{:S(2)}) collective-permute-start(bf16[2,2,8,8,128]{4,3,1,2,0:T(8,128)(2,1)S(1)} %get-tuple-element.18), channel_id=1, source_target_pairs={{1,0},{2,1},{3,2},{4,3},{5,4},{6,5},{7,6},{9,8},{10,9},{11,10},{12... | collective-permute-start | bytes 196616 | tf_op jit(solution)/shard_map/ppermute | solution.py:19
  12.3 10.0 %collective-permute-start.3 = (bf16[2,2,8,32,128]{4,3,1,2,0:T(8,128)(2,1)S(1)}, bf16[2,2,8,32,128]{4,3,1,2,0:T(8,128)(2,1)S(1)}, u32[]{:S(2)}, u32[]{:S(2)}) collective-permute-start(bf16[2,2,8,32,128]{4,3,1,2,0:T(8,128)(2,1)S(1)} %pad_maximum_fusion.2), channel_id=1, source_target_pairs={{8,0},{16,8},{24,16},{32,24},{40,32},{48,40},{56,48},{64,56},{72,6... | collective-permute-start | bytes 786440 | tf_op jit(solution)/shard_map/ppermute | solution.py:19
  19.5 5.2 %collective-permute-start.2 = (bf16[2,2,8,32,128]{4,3,1,2,0:T(8,128)(2,1)S(1)}, bf16[2,2,8,32,128]{4,3,1,2,0:T(8,128)(2,1)S(1)}, u32[]{:S(2)}, u32[]{:S(2)}) collective-permute-start(bf16[2,2,8,32,128]{4,3,1,2,0:T(8,128)(2,1)S(1)} %pad_maximum_fusion.2), channel_id=1, source_target_pairs={{0,8},{8,16},{16,24},{24,32},{32,40},{40,48},{48,56},{56,64},{64,7... | collective-permute-start | bytes 786440 | tf_op jit(solution)/shard_map/ppermute | solution.py:18
  25.1 1.1 copy-start.2
  25.2 1.1 copy-start.10
  27.7 0.7 copy-start.9
  29.7 0.7 collective-permute-start.4
  30.4 0.7 copy-start.8
  32.2 0.7 copy-start.7
  34.1 1.1 copy-start.6
  34.2 0.7 collective-permute-start.5
  35.9 0.8 copy-start.5
  37.6 16.4 %collective-permute-start.6 = (bf16[2,12,20,128]{3,2,0,1:T(8,128)(2,1)S(1)}, bf16[2,12,20,128]{3,2,0,1:T(8,128)(2,1)S(1)}, u32[]{:S(2)}, u32[]{:S(2)}) collective-permute-start(bf16[2,12,20,128]{3,2,0,1:T(8,128)(2,1)S(1)} %fusion.53), channel_id=1, source_target_pairs={{128,0},{129,1},{130,2},{131,3},{132,4},{133,5},{134,6},{135,7},{1... | collective-permute-start | bytes 368648 | tf_op jit(solution)/shard_map/ppermute | solution.py:124
  38.9 15.7 %copy-start.4 = (pred[16,3]{0,1:T(4,128)(4,1)S(1)}, pred[16,3]{0,1:T(4,128)(4,1)}, u32[]{:S(2)}) copy-start(pred[16,3]{0,1:T(4,128)(4,1)} %constant.62) | copy-start | bytes 148
  55.3 0.8 copy-start.1
  55.7 1.1 copy-start
  108.6 10.7 %all-to-all-start.2 = ((bf16[8,36,128]{2,1,0:T(8,128)(2,1)}), bf16[8,36,128]{2,1,0:T(8,128)(2,1)S(1)}, u32[]{:S(2)}, u32[]{:S(2)}) async-start(bf16[8,36,128]{2,1,0:T(8,128)(2,1)} %stack.115), calls=%async_computation.2 | async-start | bytes 163840 | tf_op jit(solution)/shard_map/all_to_all | solution.py:77
  112.2 14.4 %copy-start.3 = (pred[16,3]{0,1:T(4,128)(4,1)S(1)}, pred[16,3]{0,1:T(4,128)(4,1)}, u32[]{:S(2)}) copy-start(pred[16,3]{0,1:T(4,128)(4,1)} %constant.61) | copy-start | bytes 148
  120.2 16.3 %all-to-all-start.3 = ((bf16[8,288,128]{2,1,0:T(8,128)(2,1)}), bf16[8,288,128]{2,1,0:T(8,128)(2,1)S(1)}, u32[]{:S(2)}, u32[]{:S(2)}) async-start(bf16[8,288,128]{2,1,0:T(8,128)(2,1)} %broadcast_in_dim.41), calls=%async_computation.3 | async-start | bytes 1179648 | tf_op jit(solution)/shard_map/all_to_all | solution.py:63
